TPU v7x, 32 devices: a whole 2x2x4 slice. The times are simulated.
32 devices in a mesh: blk: 4 (over x, core), group: 8 (over z, y).
Axes of the slice: x: 2, y: 2, z: 4, core: 2. Of those that a mesh axis runs over, the one named last changes fastest.
Arguments:
- queries: bfloat16 [8, 512, 2048], P('group', 'blk'), may hold values from -300 to 300
- normed: bfloat16 [8, 512, 2048], P('group', 'blk'), may hold values from -6 to 6
- key_weight_copies: bfloat16 [8, 2048, 512], P('group', 'blk'), may hold values from -0.125 to 0.125
- value_weight_copies: bfloat16 [8, 2048, 512], P('group', 'blk'), may hold values from -0.125 to 0.125
- owner: int32 [4], replicated, may hold values from 0 to 7
Outputs:
- cache_keys: bfloat16 [8, 512, 512], P('group', 'blk')
- cache_values: bfloat16 [8, 512, 512], P('group', 'blk')
- attended: bfloat16 [8, 512, 2048], P('group', 'blk')
Inputs may be any that keep to these rules, and one draw needn't show every extreme that they name: `owner`: learner group index of each block of projection rows, below the number of actor groups.
All inputs are finite; a program needn't handle non-finite values.
Results may differ from a plain program's by a relative error of at most 0.011.
Values may be sent and summed in bfloat16 or wider, within the bound.
A program may use at most 64 MiB of HBM per device.

v0:
```python
import math
import jax
import jax.numpy as jnp
from jax import lax
from jax.sharding import PartitionSpec as P

QUERY_HEADS = 16
KEY_VALUE_HEADS = 4
HEAD_SIZE = 128


def spread(value, axis, source):
    kept = jnp.where(lax.axis_index(axis) == source, value, 0).astype(value.dtype)
    return lax.psum(kept, axis)


def rotate(unshaped_rows, positions):
    half_dim = HEAD_SIZE // 2
    inverse_freq = jnp.exp(
        jnp.arange(half_dim).astype(jnp.float32) * (-2.0 * math.log(500000.0) / HEAD_SIZE)
    )
    angles = positions.astype(jnp.float32)[:, None] * inverse_freq[None, :]
    cos_table = jnp.cos(angles)[:, None, :]
    sin_table = jnp.sin(angles)[:, None, :]
    reshaped_rows = unshaped_rows.reshape(unshaped_rows.shape[0], KEY_VALUE_HEADS, HEAD_SIZE)
    first_half = reshaped_rows[..., :half_dim]
    second_half = reshaped_rows[..., half_dim:]
    transposed_rows = jnp.concatenate(
        [
            first_half * cos_table - second_half * sin_table,
            second_half * cos_table + first_half * sin_table,
        ],
        axis=-1,
    )
    return transposed_rows.reshape(unshaped_rows.shape[0], KEY_VALUE_HEADS * HEAD_SIZE)


def body(queries, normed, key_weight_copies, value_weight_copies, owner):
    input_rows = normed[0]
    token_rows = input_rows.shape[0]
    owner_group = lax.dynamic_index_in_dim(owner, lax.axis_index("blk"), 0, keepdims=False)
    shard_keys, shard_values = (
        spread(key_weight_copies[0], "group", owner_group),
        spread(value_weight_copies[0], "group", owner_group),
    )
    pieces = (
        lax.all_gather(shard_keys, "blk", axis=0, tiled=True),
        lax.all_gather(shard_values, "blk", axis=0, tiled=True),
    )
    key_raw = jnp.dot(input_rows, pieces[0], preferred_element_type=jnp.float32)
    value_raw = jnp.dot(input_rows, pieces[1], preferred_element_type=jnp.float32)
    positions = lax.axis_index("blk") * token_rows + jnp.arange(token_rows, dtype=jnp.int32)
    cache_keys = rotate(key_raw, positions).astype(jnp.bfloat16)
    cache_values = value_raw.astype(jnp.bfloat16)
    query_head_grid = queries[0].reshape(
        token_rows, KEY_VALUE_HEADS, QUERY_HEADS // KEY_VALUE_HEADS, HEAD_SIZE
    )
    score_scale = HEAD_SIZE ** (-0.5)
    start_state = (
        jnp.full((KEY_VALUE_HEADS, QUERY_HEADS // KEY_VALUE_HEADS, token_rows), -1e30, jnp.float32),
        jnp.zeros((KEY_VALUE_HEADS, QUERY_HEADS // KEY_VALUE_HEADS, token_rows), jnp.float32),
        jnp.zeros(
            (KEY_VALUE_HEADS, QUERY_HEADS // KEY_VALUE_HEADS, token_rows, HEAD_SIZE), jnp.float32
        ),
    )
    pieces = (
        lax.all_gather(cache_keys, "blk", axis=0, tiled=True),
        lax.all_gather(cache_values, "blk", axis=0, tiled=True),
    )
    key_count = pieces[0].shape[0]
    key_row_width = math.gcd(key_count, 512)

    def one_block(block_turn, state_in):
        row_top, row_total, weighted_values = state_in
        offset = block_turn * key_row_width
        key_part = lax.dynamic_slice_in_dim(pieces[0], offset, key_row_width, 0).reshape(
            key_row_width, KEY_VALUE_HEADS, HEAD_SIZE
        )
        value_part = lax.dynamic_slice_in_dim(pieces[1], offset, key_row_width, 0).reshape(
            key_row_width, KEY_VALUE_HEADS, HEAD_SIZE
        )
        scores = (
            jnp.einsum(
                "lewc,jec->ewlj", query_head_grid, key_part, preferred_element_type=jnp.float32
            )
            * score_scale
        )
        key_pos = offset + jnp.arange(key_row_width, dtype=jnp.int32)
        allowed = key_pos[None, :] <= positions[:, None]
        scores = jnp.where(allowed, scores, -jnp.inf)
        new_top = jnp.maximum(row_top, jnp.max(scores, axis=-1))
        fade_by = jnp.exp(row_top - new_top)
        prob_block = jnp.exp(scores - new_top[..., None])
        row_total = row_total * fade_by + jnp.sum(prob_block, axis=-1)
        weighted_values = weighted_values * fade_by[..., None] + jnp.einsum(
            "lxbp,plj->lxbj",
            prob_block.astype(jnp.bfloat16),
            value_part,
            preferred_element_type=jnp.float32,
        )
        return (new_top, row_total, weighted_values)

    row_top, row_total, weighted_values = lax.fori_loop(
        0, key_count // key_row_width, one_block, start_state
    )
    attended = (
        (weighted_values / row_total[..., None])
        .transpose(2, 0, 1, 3)
        .reshape(token_rows, QUERY_HEADS * HEAD_SIZE)
        .astype(jnp.bfloat16)
    )
    return (cache_keys[None], cache_values[None], attended[None])


def solution(mesh):
    placed = (
        P("group", "blk", None),
        P("group", "blk", None),
        P("group", "blk", None),
        P("group", "blk", None),
        P(),
    )
    return jax.shard_map(
        body,
        mesh=mesh,
        in_specs=placed,
        out_specs=(P("group", "blk", None), P("group", "blk", None), P("group", "blk", None)),
        check_vma=False,
    )
```

profile of v0, /device:TPU:0, one launch (start us, length us, event | category | flops | bytes accessed | tf_op | source)
XLA Modules:
  0.0 169.3 jit_solution(15250934654074469088)
XLA Ops:
  7.2 0.0 copy-start
  7.2 0.0 copy-start.1
  7.2 0.0 all-reduce.3.cloned.1.call-start
  7.2 1.3 dynamic_slice.8
  9.2 1.1 select_bitcast_fusion
  10.3 0.0 all-reduce.3.cloned.1.call-update
  10.3 0.0 all-gather.5.cloned.1.call-start
  10.4 82.8 %all-reduce.3.cloned.1.call-done = (bf16[512,512]{1,0:T(8,128)(2,1)}, bf16[512,512]{1,0:T(8,128)(2,1)}) async-done(((bf16[512,512]{1,0:T(8,128)(2,1)}, bf16[512,512]{1,0:T(8,128)(2,1)}), (bf16[512,512]{1,0:T(8,128)(2,1)}, bf16[512,512]{1,0:T(8,128)(2,1)})) %all-reduce.3.cloned.1.call-update) | async-done | bytes 1048592 | tf_op jit(solution)/shard_map/psum | solution.py:14
  93.1 0.0 all-gather.5.cloned.1.call-update
  93.2 0.0 all-gather.3.cloned.1.call-start
  93.2 0.7 all-gather.3.cloned.1.call-update
  93.9 0.0 copy-done.1
  93.9 0.4 reshape_squeeze.3
  94.4 0.2 multiply_cosine_fusion
  94.6 22.3 %all-gather.5.cloned.1.call-done = bf16[2048,512]{1,0:T(8,128)(2,1)} async-done(((bf16[512,512]{1,0:T(8,128)(2,1)}), bf16[2048,512]{1,0:T(8,128)(2,1)}) %all-gather.5.cloned.1.call-update) | async-done | bytes 2097168 | tf_op jit(solution)/shard_map/all_gather | solution.py:48
  116.9 0.0 copy-done
  116.9 2.3 %convolution_convert_fusion = bf16[512,128]{1,0:T(8,128)(2,1)S(1)} fusion(bf16[2048,512]{1,0:T(8,128)(2,1)} %all-gather.5.cloned.1.call-done, bf16[1,128,2048]{2,1,0:T(8,128)(2,1)S(1)} %copy-done), kind=kOutput, calls=%fused_computation.12 | convolution fusion | flops 268500992 | bytes 2752512 | tf_op jit(solution)/shard_map/dot_general | solution.py:51
  119.3 0.8 copy.17
  120.0 21.0 %all-gather.3.cloned.1.call-done = bf16[2048,512]{1,0:T(8,128)(2,1)} async-done(((bf16[512,512]{1,0:T(8,128)(2,1)}), bf16[2048,512]{1,0:T(8,128)(2,1)}) %all-gather.3.cloned.1.call-update) | async-done | bytes 2097168 | tf_op jit(solution)/shard_map/all_gather | solution.py:47
  141.1 2.3 %fusion.18 = f32[512,128]{1,0:T(8,128)S(1)} fusion(bf16[2048,512]{1,0:T(8,128)(2,1)} %all-gather.3.cloned.1.call-done, bf16[1,128,2048]{2,1,0:T(8,128)(2,1)S(1)} %copy-done), kind=kOutput, calls=%fused_computation.15 | convolution fusion | flops 268435456 | bytes 2883584 | tf_op jit(solution)/shard_map/dot_general | solution.py:50
  143.5 0.8 copy.22
  144.3 7.2 %all_gather.15 = bf16[512,512]{0,1:T(8,128)(2,1)S(1)} all-gather(bf16[128,512]{0,1:T(8,128)(2,1)S(1)} %bitcast.64), channel_id=1, replica_groups=mesh['blk'=4,'group'=8] {'blk'}, dimensions={0}, use_global_device_ids=true | all-gather | bytes 655360 | tf_op jit(solution)/shard_map/all_gather | solution.py:68
  151.4 7.3 %all_gather.14 = bf16[512,512]{0,1:T(8,128)(2,1)S(1)} all-gather(bf16[128,512]{0,1:T(8,128)(2,1)S(1)} %bitcast.62), channel_id=1, replica_groups=mesh['blk'=4,'group'=8] {'blk'}, dimensions={0}, use_global_device_ids=true | all-gather | bytes 655360 | tf_op jit(solution)/shard_map/all_gather | solution.py:67
  158.7 0.9 fusion.2
  159.6 0.9 fusion
  160.5 1.2 divide_convert_fusion
  161.7 1.0 copy.18
  (8 shorter events, 0.1 us)
Async XLA Ops:
  7.2 109.8 %copy-start = (bf16[1,128,2048]{2,1,0:T(8,128)(2,1)S(1)}, bf16[1,128,2048]{2,1,0:T(8,128)(2,1)}, u32[]{:S(2)}) copy-start(bf16[1,128,2048]{2,1,0:T(8,128)(2,1)} %param.6) | copy-start | bytes 1572868
  7.2 86.7 %copy-start.1 = (bf16[1,128,2048]{2,1,0:T(8,128)(2,1)S(1)}, bf16[1,128,2048]{2,1,0:T(8,128)(2,1)}, u32[]{:S(2)}) copy-start(bf16[1,128,2048]{2,1,0:T(8,128)(2,1)} %param.5) | copy-start | bytes 1572868
  7.2 86.0 %all-reduce.3.cloned.1.call-start = ((), (), s32[]{:S(2)}) async-start(), calls=%async_computation.2 | async-start | bytes 2097152 | tf_op jit(solution)/shard_map/psum | solution.py:14
  10.3 106.6 %all-gather.5.cloned.1.call-start = ((), (), s32[]{:S(2)}) async-start(), calls=%async_computation.1 | async-start | bytes 2621440 | tf_op jit(solution)/shard_map/all_gather | solution.py:48
  93.2 47.9 %all-gather.3.cloned.1.call-start = ((), (), s32[]{:S(2)}) async-start(), calls=%async_computation | async-start | bytes 2621440 | tf_op jit(solution)/shard_map/all_gather | solution.py:47
Sparse Core Ops, SparseCore 0:
  12.1 80.9 all-reduce.2
  94.7 22.1 all-gather.4
  118.5 22.5 all-gather.2
where the time goes:
time: 169 us
  waiting for transfers between devices  127 us (75%)
  blocking collectives  14.5 us (9%)
  between operations  14.5 us (9%)
  matrix products  6.72 us (4%)
  local copies, waits for them, and re-layouts  4.27 us (3%)
  other arithmetic  2.28 us (1%)
    psum x1, waiting for transfers between devices, spread(): return lax.psum(kept, axis)  82.8 us
    all_gather x1, waiting for transfers between devices, body(): lax.all_gather(shard_values, 'blk', axis=0, tiled=True)  22.3 us
    all_gather x1, waiting for transfers between devices, body(): lax.all_gather(shard_keys, 'blk', axis=0, tiled=True)  21 us
    all_gather x1, blocking collectives, body(): lax.all_gather(cache_keys, 'blk', axis=0, tiled=True)  7.29 us
    all_gather x1, blocking collectives, body(): lax.all_gather(cache_values, 'blk', axis=0, tiled=True)  7.18 us
  transfers between devices with their start and end apart: 3, of which 3 were waited for; matrix products, arithmetic and copies ran while one was open for 2% of the time, Pallas kernels for 0%

commit v1 on v0

--- a/solution.py
+++ b/solution.py
@@ -9,9 +9,15 @@
 HEAD_SIZE = 128
 
 
+def gather_and_add(x, axis):
+    parts = lax.all_gather(x, axis, axis=0, tiled=False)
+    summed = parts.sum(axis=0)
+    return summed
+
+
 def spread(value, axis, source):
     kept = jnp.where(lax.axis_index(axis) == source, value, 0).astype(value.dtype)
-    return lax.psum(kept, axis)
+    return gather_and_add(kept, axis)
 
 
 def rotate(unshaped_rows, positions):

time: 169 us -> 235 us (1.39)
  waiting for transfers between devices: 127 us -> 185 us
  other arithmetic: 2.28 us -> 10.4 us
    all_gather x0 -> x2, waiting for transfers between devices: none -> 145 us  [gather_and_add(): parts = lax.all_gather(x, axis, axis=0, tiled=False)]
    psum x1 -> x0, waiting for transfers between devices: 82.8 us -> none  [spread(): return lax.psum(kept, axis)]
    reduce_sum x0 -> x2, other arithmetic: none -> 7.47 us  [gather_and_add(): summed = parts.sum(axis=0)]
  transfers between devices with their start and end apart: 3 -> 4, of which waited for: 3 -> 4; matrix products, arithmetic and copies ran while one was open for 2% -> 5% of each run, Pallas kernels for 0% -> 0%
where the time goes in v1:
time: 235 us
  waiting for transfers between devices  185 us (79%)
  blocking collectives  14.5 us (6%)
  between operations  14.5 us (6%)
  other arithmetic  10.4 us (4%)
  matrix products  6.72 us (3%)
  local copies, waits for them, and re-layouts  4.22 us (2%)
    all_gather x2, waiting for transfers between devices, gather_and_add(): parts = lax.all_gather(x, axis, axis=0, tiled=False)  145 us
    all_gather x1, waiting for transfers between devices, body(): lax.all_gather(shard_values, 'blk', axis=0, tiled=True)  20.8 us
    all_gather x1, waiting for transfers between devices, body(): lax.all_gather(shard_keys, 'blk', axis=0, tiled=True)  18.8 us
    reduce_sum x2, other arithmetic, gather_and_add(): summed = parts.sum(axis=0)  7.47 us
    all_gather x1, blocking collectives, body(): lax.all_gather(cache_keys, 'blk', axis=0, tiled=True)  7.29 us
    all_gather x1, blocking collectives, body(): lax.all_gather(cache_values, 'blk', axis=0, tiled=True)  7.18 us
  transfers between devices with their start and end apart: 4, of which 4 were waited for; matrix products, arithmetic and copies ran while one was open for 5% of the time, Pallas kernels for 0%

profile of v1, /device:TPU:0, one launch (start us, length us, event | category | flops | bytes accessed | tf_op | source)
XLA Modules:
  0.0 235.1 jit_solution(17581424227489117133)
XLA Ops:
  7.2 0.0 copy-start
  7.2 0.0 all-gather.5.cloned.1.call-start
  7.2 1.3 dynamic_slice.8
  9.2 0.8 broadcast_select_fusion.1
  10.0 0.0 all-gather.5.cloned.1.call-update
  10.0 0.0 all-gather.9.cloned.1.call-start
  10.1 0.9 broadcast_select_fusion
  11.0 0.0 all-gather.9.cloned.1.call-update
  11.0 0.0 copy-start.1
  11.0 0.0 all-gather.7.cloned.1.call-start
  11.1 75.2 %all-gather.5.cloned.1.call-done = bf16[8,512,512]{2,1,0:T(8,128)(2,1)} async-done(((bf16[1,512,512]{2,1,0:T(8,128)(2,1)}), bf16[8,512,512]{2,1,0:T(8,128)(2,1)}) %all-gather.5.cloned.1.call-update) | async-done | bytes 4194320 | tf_op jit(solution)/shard_map/all_gather | solution.py:13
  86.2 3.7 %reduce_sum.36 = bf16[512,512]{1,0:T(8,128)(2,1)} reduce(bf16[8,512,512]{2,1,0:T(8,128)(2,1)} %all-gather.5.cloned.1.call-done, bf16[]{:T(256)} %constant.38.clone.1), dimensions={0}, to_apply=%region_0.1 | reduce | flops 1835008 | bytes 4718594 | tf_op jit(solution)/shard_map/reduce_sum | solution.py:14
  90.0 0.0 all-gather.7.cloned.1.call-update
  90.0 0.0 all-gather.11.cloned.1.call-start
  90.0 69.7 %all-gather.9.cloned.1.call-done = bf16[8,512,512]{2,1,0:T(8,128)(2,1)} async-done(((bf16[1,512,512]{2,1,0:T(8,128)(2,1)}), bf16[8,512,512]{2,1,0:T(8,128)(2,1)}) %all-gather.9.cloned.1.call-update) | async-done | bytes 4194320 | tf_op jit(solution)/shard_map/all_gather | solution.py:13
  159.7 3.7 %reduce_sum.37 = bf16[512,512]{1,0:T(8,128)(2,1)} reduce(bf16[8,512,512]{2,1,0:T(8,128)(2,1)} %all-gather.9.cloned.1.call-done, bf16[]{:T(256)} %constant.38.clone.1), dimensions={0}, to_apply=%region_1.2 | reduce | flops 1835008 | bytes 4718594 | tf_op jit(solution)/shard_map/reduce_sum | solution.py:14
  163.5 0.0 all-gather.11.cloned.1.call-update
  163.5 0.0 copy-done.1
  163.5 0.4 reshape_squeeze.3
  164.0 0.2 multiply_cosine_fusion
  164.2 18.8 %all-gather.7.cloned.1.call-done = bf16[2048,512]{1,0:T(8,128)(2,1)} async-done(((bf16[512,512]{1,0:T(8,128)(2,1)}), bf16[2048,512]{1,0:T(8,128)(2,1)}) %all-gather.7.cloned.1.call-update) | async-done | bytes 2097168 | tf_op jit(solution)/shard_map/all_gather | solution.py:53
  183.0 2.3 fusion.18
  185.4 0.8 copy.28
  186.2 20.8 %all-gather.11.cloned.1.call-done = bf16[2048,512]{1,0:T(8,128)(2,1)} async-done(((bf16[512,512]{1,0:T(8,128)(2,1)}), bf16[2048,512]{1,0:T(8,128)(2,1)}) %all-gather.11.cloned.1.call-update) | async-done | bytes 2097168 | tf_op jit(solution)/shard_map/all_gather | solution.py:54
  207.0 2.3 convolution_convert_fusion
  209.3 0.8 copy.23
  210.1 7.2 %all_gather.25 = bf16[512,512]{0,1:T(8,128)(2,1)S(1)} all-gather(bf16[128,512]{0,1:T(8,128)(2,1)S(1)} %bitcast.60), channel_id=1, replica_groups=mesh['blk'=4,'group'=8] {'blk'}, dimensions={0}, use_global_device_ids=true | all-gather | bytes 655360 | tf_op jit(solution)/shard_map/all_gather | solution.py:74
  217.3 7.3 %all_gather.24 = bf16[512,512]{0,1:T(8,128)(2,1)S(1)} all-gather(bf16[128,512]{0,1:T(8,128)(2,1)S(1)} %bitcast.58), channel_id=1, replica_groups=mesh['blk'=4,'group'=8] {'blk'}, dimensions={0}, use_global_device_ids=true | all-gather | bytes 655360 | tf_op jit(solution)/shard_map/all_gather | solution.py:73
  224.6 0.9 fusion.2
  225.5 0.9 fusion
  226.4 1.2 divide_convert_fusion
  227.6 1.0 copy.24
  (9 shorter events, 0.1 us)
Async XLA Ops:
  7.2 175.8 %copy-start = (bf16[1,128,2048]{2,1,0:T(8,128)(2,1)S(1)}, bf16[1,128,2048]{2,1,0:T(8,128)(2,1)}, u32[]{:S(2)}) copy-start(bf16[1,128,2048]{2,1,0:T(8,128)(2,1)} %param.6) | copy-start | bytes 1572868
  7.2 79.1 %all-gather.5.cloned.1.call-start = ((), (), s32[]{:S(2)}) async-start(), calls=%async_computation | async-start | bytes 4718592 | tf_op jit(solution)/shard_map/all_gather | solution.py:13
  10.0 149.7 %all-gather.9.cloned.1.call-start = ((), (), s32[]{:S(2)}) async-start(), calls=%async_computation.2 | async-start | bytes 4718592 | tf_op jit(solution)/shard_map/all_gather | solution.py:13
  11.0 152.5 %copy-start.1 = (bf16[1,128,2048]{2,1,0:T(8,128)(2,1)S(1)}, bf16[1,128,2048]{2,1,0:T(8,128)(2,1)}, u32[]{:S(2)}) copy-start(bf16[1,128,2048]{2,1,0:T(8,128)(2,1)} %param.5) | copy-start | bytes 1572868
  11.0 172.0 %all-gather.7.cloned.1.call-start = ((), (), s32[]{:S(2)}) async-start(), calls=%async_computation.1 | async-start | bytes 2621440 | tf_op jit(solution)/shard_map/all_gather | solution.py:53
  90.0 117.0 %all-gather.11.cloned.1.call-start = ((), (), s32[]{:S(2)}) async-start(), calls=%async_computation.3 | async-start | bytes 2621440 | tf_op jit(solution)/shard_map/all_gather | solution.py:54
Sparse Core Ops, SparseCore 0:
  10.7 75.5 all-gather.4
  88.4 71.3 all-gather.8
  161.9 21.0 all-gather.6
  184.4 22.5 all-gather.10
